TPU v7x, 32 devices: a whole 2x2x4 slice. The times are simulated.
32 devices in a mesh: gx: 2 (over x), gy: 4 (over z), gz: 4 (over y, core).
Axes of the slice: x: 2, y: 2, z: 4, core: 2. Of those that a mesh axis runs over, the one named last changes fastest.
Arguments:
- body_load: float32 [3, 8, 64, 512], P(None, 'gx', 'gy', 'gz'), may hold values from -24 to 24
- contact_mask: int32 [8, 64, 512], P('gx', 'gy', 'gz'), may hold values 0 or 1
- contact_gap: float32 [8, 64, 512], P('gx', 'gy', 'gz'), may hold values from 0.1 to 0.8
- material_ids: int32 [8, 64, 512], P('gx', 'gy', 'gz'), may hold values from 0 to 3
- lame_table: float32 [4, 2], replicated, may hold values from 0.5 to 2
Outputs:
- displacement: float32 [3, 8, 64, 512], P(None, 'gx', 'gy', 'gz')
- multiplier: float32 [3, 8, 64, 512], P(None, 'gx', 'gy', 'gz')
- gap_history: float32 [6], replicated
All inputs are finite; a program needn't handle non-finite values. No bound on the sum of `contact_mask` on one device may be relied on, other than what follows from the above.
Results may differ from a plain program's by a relative error of at most 0.0001.
Values sent between devices are 32-bit elements; how exact they have to be, the bound alone decides.
A program may use at most 64 MiB of HBM per device.

v0:
```python
import functools

import jax
import jax.numpy as jnp
import numpy as np
from jax import lax
from jax.experimental import pallas as pl
from jax.experimental.pallas import tpu as pltpu
from jax.sharding import PartitionSpec as P

ITERS = 6
DEPTHS = (1, 1, 1, 1, 1)
AXES = ("gx", "gy", "gz")
MESH = pl.DeviceIdType.MESH
DIRS = [
    (dx, dy, dz) for dx in (-1, 0, 1) for dy in (-1, 0, 1) for dz in (-1, 0, 1) if (dx, dy, dz) != (0, 0, 0)
]
DIRS.sort(key=lambda k: -sum(abs(a) for a in k))


def corner_offsets(a):
    return (a >> 2 & 1, a >> 1 & 1, a & 1)


def element_tables():
    points = np.array([(1.0 - 3.0 ** (-0.5)) / 2.0, (1.0 + 3.0 ** (-0.5)) / 2.0])
    stiff_lame = np.zeros((24, 24))
    stiff_shear = np.zeros((24, 24))
    for p in points:
        for q in points:
            for r in points:
                position = (p, q, r)
                gradients = np.zeros((8, 3))
                for a in range(8):
                    corner = corner_offsets(a)
                    for d in range(3):
                        factor = 1.0
                        for e in range(3):
                            if e == d:
                                factor = factor * (1.0 if corner[e] else -1.0)
                            else:
                                factor = factor * (position[e] if corner[e] else 1.0 - position[e])
                        gradients[a, d] = factor
                for a in range(8):
                    for c in range(3):
                        for b in range(8):
                            for d in range(3):
                                stiff_lame[3 * a + c, 3 * b + d] += 0.125 * gradients[a, c] * gradients[b, d]
                                stiff_shear[3 * a + c, 3 * b + d] += 0.125 * (
                                    float(c == d) * np.dot(gradients[a], gradients[b])
                                    + gradients[a, d] * gradients[b, c]
                                )
    return (stiff_lame, stiff_shear)


def element_modes(m, L, M):
    x, y, z = m
    M2 = M + M
    L3 = L * (1.0 / 3.0)
    M3 = M * (1.0 / 3.0)
    Q = (L + (M2 + M2)) * (1.0 / 9.0)
    s = L * (x["DSS"] + y["SDS"] + z["SSD"])
    fx, fy, fz = {}, {}, {}
    fx["DSS"] = s + M2 * x["DSS"]
    fy["SDS"] = s + M2 * y["SDS"]
    fz["SSD"] = s + M2 * z["SSD"]
    fy["DSS"] = fx["SDS"] = M * (y["DSS"] + x["SDS"])
    fz["DSS"] = fx["SSD"] = M * (z["DSS"] + x["SSD"])
    fz["SDS"] = fy["SSD"] = M * (z["SDS"] + y["SSD"])
    ax = L3 * (y["DDS"] + z["DSD"])
    ay = L3 * (x["DDS"] + z["SDD"])
    az = L3 * (x["DSD"] + y["SDD"])
    fx["DDS"] = ay + M * x["DDS"]
    fx["DSD"] = az + M * x["DSD"]
    fy["DDS"] = ax + M * y["DDS"]
    fy["SDD"] = az + M * y["SDD"]
    fz["DSD"] = ax + M * z["DSD"]
    fz["SDD"] = ay + M * z["SDD"]
    p = M3 * (y["DSD"] + x["SDD"])
    q = M3 * (x["SDD"] + z["DDS"])
    r = M3 * (y["DSD"] + z["DDS"])
    fx["SDD"] = p + q
    fy["DSD"] = p + r
    fz["DDS"] = q + r
    for f, v in ((fx, x), (fy, y), (fz, z)):
        f["DDD"] = Q * v["DDD"]
    return fx, fy, fz


YZ = ("SS", "SD", "DS", "DD")


def plane_modes(v):
    rows, lanes = v.shape
    nz = pltpu.roll(v, lanes - 1, 1)
    s, d = v + nz, nz - v
    s1, d1 = pltpu.roll(s, rows - 1, 0), pltpu.roll(d, rows - 1, 0)
    return [s + s1, d + d1, s1 - s, d1 - d]


def plane_forces(g):
    B = []
    for zm in (0, 1):
        S, D = g[zm], g[2 + zm]
        B.append((S - D) + pltpu.roll(S + D, 1, 0))
    return (B[0] - B[1]) + pltpu.roll(B[0] + B[1], 1, 1)


def make_kernel(counts, brick, nmat, gl, gm):
    bx, by, bz = counts_brick = brick
    H = max(DEPTHS)
    rounds = len(DEPTHS)
    total = counts[0] * counts[1] * counts[2]
    nfields = [5] + [3 if d == 1 else 5 for d in DEPTHS[1:]]
    YW = by + 8
    ZW = 2 * bz

    def kernel(*refs):
        body, mask, gap, mat, lame, u_out, w_out, gap_out = refs[:8]
        Rs = refs[8 : 8 + rounds]
        Ps = refs[8 + rounds : 8 + 2 * rounds]
        (U, W, N, B, LOW, LL, MM, GA, GT, GR, send, recv, gsend, grecv) = refs[8 + 2 * rounds :]
        me = [lax.axis_index(a) for a in AXES]

        def peer(offset):
            return tuple(lax.rem(me[i] + offset[i] + counts[i], counts[i]) for i in range(3))

        def unravel(j):
            a = j // (counts[1] * counts[2])
            b = (j // counts[2]) % counts[1]
            return (a, b, j % counts[2])

        barrier = pltpu.get_barrier_semaphore()

        @pl.loop(1, total)
        def _(j):
            pl.semaphore_signal(barrier, inc=1, device_id=peer(unravel(j)), device_id_type=MESH)

        lane = lax.broadcasted_iota(jnp.int32, (by, bz), 1)
        lane8 = lax.broadcasted_iota(jnp.int32, (YW, bz), 1)

        def fill(r, fields):
            d = DEPTHS[r]
            for x in range(bx):
                packed = None
                for f, field in enumerate(fields):
                    v = field(x)
                    Rs[r][f, d + x, 8 : 8 + by, :] = v
                    shifted = pltpu.roll(v, 2 * d * f + d, 1)
                    packed = shifted if packed is None else jnp.where(lane >= 2 * d * f, shifted, packed)
                Ps[r][0, d + x, 8 : 8 + by, :] = packed

        def copies(r):
            d = DEPTHS[r]
            for k, (dx, dy, dz) in enumerate(DIRS):
                sx = pl.ds(bx, d) if dx > 0 else pl.ds(d, d if dx else bx)
                tx = pl.ds(0, d) if dx > 0 else (pl.ds(d + bx, d) if dx else pl.ds(d, bx))
                sy = pl.ds(by, 8) if dy > 0 else pl.ds(8, 8 if dy else by)
                ty = pl.ds(0, 8) if dy > 0 else (pl.ds(8 + by, 8) if dy else pl.ds(8, by))
                if dz == 0:
                    src, dst = Rs[r].at[:, sx, sy, :], Rs[r].at[:, tx, ty, :]
                else:
                    src, dst = Ps[r].at[0, sx, sy, :], Ps[r].at[1 if dz > 0 else 2, tx, ty, :]
                yield pltpu.make_async_remote_copy(
                    src_ref=src,
                    dst_ref=dst,
                    send_sem=send.at[r, k],
                    recv_sem=recv.at[r, k],
                    device_id=peer((dx, dy, dz)),
                    device_id_type=MESH,
                )

        def unpack(r, x, f):
            d = DEPTHS[r]
            rows = pl.ds(4, YW)
            own = Rs[r][f, x, rows, :]
            both = jnp.where(lane8 % (2 * d) < d, Ps[r][1, x, rows, :], Ps[r][2, x, rows, :])
            return jnp.concatenate([own, pltpu.roll(both, (bz - (2 * d * f + d)) % bz, 1)], 1)

        top = None
        for m in range(nmat):
            row = lame[m, 0] * gl + lame[m, 1] * gm
            top = row if top is None else jnp.maximum(top, row)
        tau = 1.5 / jnp.full((YW, ZW), 1.0 + 8.0 * top, jnp.float32)

        fill(
            0,
            [
                lambda x: body[0, x],
                lambda x: body[1, x],
                lambda x: body[2, x],
                lambda x: jnp.where(mask[x] > 0, -gap[x], -jnp.inf),
                lambda x: mat[x].astype(jnp.float32),
            ],
        )
        GT[...] = jnp.zeros_like(GT)
        pl.semaphore_wait(barrier, total - 1)

        def settle(x, u, w, low):
            worst = None
            for c in range(3):
                v = u[c] + w[c]
                z = jnp.maximum(v, low) if c == 2 else v
                wc = v - z
                res = u[c] - z
                U[c, x], W[c, x], N[c, x] = u[c], wc, res + wc
                a = jnp.abs(res[:, :bz])
                worst = a if worst is None else jnp.maximum(worst, a)
            inside = jnp.logical_and(x >= H, x < H + bx)
            GA[...] = jnp.maximum(GA[...], jnp.where(inside, worst, 0.0))

        def record(t):
            GT[t : t + 1, :] = jnp.max(GA[4 : 4 + by, :], axis=0, keepdims=True)

        t = 0
        for r, d in enumerate(DEPTHS):
            if r > 0:
                own = (pl.ds(4, by), pl.ds(0, bz))
                fields = [lambda x, c=c: U[c, H + x, own[0], own[1]] for c in range(3)]
                if d > 1:
                    fields += [
                        lambda x: W[2, H + x, own[0], own[1]],
                        lambda x: N[2, H + x, own[0], own[1]],
                    ]
                fill(r, fields)
            for copy in copies(r):
                copy.start()
            for copy in copies(r):
                copy.wait_recv()
            if r == 0:
                GA[...] = jnp.zeros_like(GA)

                @pl.loop(0, bx + 2 * H)
                def _(x):
                    u = []
                    for c in range(3):
                        b = tau * unpack(0, x, c)
                        B[c, x] = b
                        u.append(b)
                    low = unpack(0, x, 3)
                    LOW[x] = low
                    kind = unpack(0, x, 4)
                    first = jnp.zeros_like(kind)
                    shear = jnp.zeros_like(kind)
                    for m in range(nmat):
                        hit = kind == float(m)
                        first = jnp.where(hit, lame[m, 0], first)
                        shear = jnp.where(hit, lame[m, 1], shear)
                    LL[x] = first * (tau * 0.0625)
                    MM[x] = shear * (tau * 0.0625)
                    zero = jnp.zeros_like(kind)
                    settle(x, u, [zero, zero, zero], low)

                record(0)
                t = 1
            else:

                @pl.loop(0, bx + 2 * d)
                def _(x):
                    for c in range(3):
                        U[c, x + H - d] = unpack(r, x, c)
                    if d > 1:
                        W[2, x + H - d] = unpack(r, x, 3)
                        N[2, x + H - d] = unpack(r, x, 4)

            for left in range(d, 0, -1):
                GA[...] = jnp.zeros_like(GA)
                start = H - left

                def step(e, carry):
                    prev, hi = carry
                    cur = [plane_modes(U[c, e + 1]) for c in range(3)]
                    modes = []
                    for c in range(3):
                        m = {}
                        for i, yz in enumerate(YZ):
                            a, b = prev[4 * c + i], cur[c][i]
                            m["D" + yz] = b - a
                            if yz != "SS":
                                m["S" + yz] = a + b
                        modes.append(m)
                    forces = element_modes(modes, LL[e], MM[e])
                    new_hi, u, w = [], [], []
                    for c in range(3):
                        g = []
                        for i, yz in enumerate(YZ):
                            D = forces[c]["D" + yz]
                            h = hi[4 * c + i]
                            if yz == "SS":
                                g.append(h - D)
                                new_hi.append(D)
                            else:
                                S = forces[c]["S" + yz]
                                g.append(h + (S - D))
                                new_hi.append(S + D)
                        F = plane_forces(g)
                        u.append(U[c, e] - ((F - B[c, e]) + tau * N[c, e]))
                        w.append(W[c, e])
                    settle(e, u, w, LOW[e])
                    return [v for c in cur for v in c], new_hi

                zero = jnp.zeros((YW, ZW), jnp.float32)
                carry = ([v for c in range(3) for v in plane_modes(U[c, start])], [zero] * 12)
                lax.fori_loop(start, H + bx - 1 + left, step, carry)
                record(t)
                t += 1

        for c in range(3):
            for x in range(bx):
                u_out[c, x] = U[c, H + x, 4 : 4 + by, :bz]
                w_out[c, x] = W[c, H + x, 4 : 4 + by, :bz]

        @pl.loop(1, total)
        def _(j):
            pltpu.make_async_remote_copy(
                src_ref=GT,
                dst_ref=GR.at[j - 1],
                send_sem=gsend,
                recv_sem=grecv,
                device_id=peer(unravel(j)),
                device_id_type=MESH,
            ).start()

        whole = pltpu.make_async_remote_copy(
            src_ref=GR,
            dst_ref=GR,
            send_sem=gsend,
            recv_sem=grecv,
            device_id=peer((0, 0, 1)),
            device_id_type=MESH,
        )
        whole.wait_recv()
        worst = jnp.maximum(GT[...], jnp.max(GR[...], axis=0))
        for i in range(ITERS):
            gap_out[i] = jnp.max(worst[i : i + 1, :])
        whole.wait_send()
        for r in range(rounds):
            for copy in copies(r):
                copy.wait_send()

    X = bx + 2 * H
    plane = lambda *lead: pltpu.VMEM(lead + (X, YW, ZW), jnp.float32)
    scratch = [
        pltpu.VMEM((n, bx + 2 * d, by + 16, bz), jnp.float32) for n, d in zip(nfields, DEPTHS)
    ]
    scratch += [pltpu.VMEM((3, bx + 2 * d, by + 16, bz), jnp.float32) for d in DEPTHS]
    scratch += [plane(3), plane(3), plane(3), plane(3), plane(), plane(), plane()]
    scratch += [
        pltpu.VMEM((YW, bz), jnp.float32),
        pltpu.VMEM((8, bz), jnp.float32),
        pltpu.VMEM((total - 1, 8, bz), jnp.float32),
        pltpu.SemaphoreType.DMA((rounds, len(DIRS))),
        pltpu.SemaphoreType.DMA((rounds, len(DIRS))),
        pltpu.SemaphoreType.DMA,
        pltpu.SemaphoreType.DMA,
    ]
    return kernel, scratch


def shards(counts, body_load, contact_mask, contact_gap, material_ids, lame_table):
    stiff_lame, stiff_shear = element_tables()
    gl = float(np.max(np.sum(np.abs(stiff_lame), 1)))
    gm = float(np.max(np.sum(np.abs(stiff_shear), 1)))
    kernel, scratch = make_kernel(counts, material_ids.shape, lame_table.shape[0], gl, gm)
    vmem = pl.BlockSpec(memory_space=pltpu.VMEM)
    smem = pl.BlockSpec(memory_space=pltpu.SMEM)
    return pl.pallas_call(
        kernel,
        out_shape=(
            jax.ShapeDtypeStruct(body_load.shape, jnp.float32),
            jax.ShapeDtypeStruct(body_load.shape, jnp.float32),
            jax.ShapeDtypeStruct((ITERS,), jnp.float32),
        ),
        in_specs=[vmem] * 4 + [smem],
        out_specs=(vmem, vmem, smem),
        scratch_shapes=scratch,
        compiler_params=pltpu.CompilerParams(
            collective_id=0, has_side_effects=True, vmem_limit_bytes=48 * 1024 * 1024
        ),
    )(body_load, contact_mask, contact_gap, material_ids, lame_table)


def solution(mesh):
    counts = tuple(mesh.shape[a] for a in AXES)
    in_specs = (
        P(None, "gx", "gy", "gz"),
        P("gx", "gy", "gz"),
        P("gx", "gy", "gz"),
        P("gx", "gy", "gz"),
        P(),
    )
    out_specs = (P(None, "gx", "gy", "gz"), P(None, "gx", "gy", "gz"), P())
    return jax.shard_map(
        functools.partial(shards, counts), mesh=mesh, in_specs=in_specs, out_specs=out_specs, check_vma=False
    )
```

profile of v0, /device:TPU:0, one launch (start us, length us, event | category | flops | bytes accessed | tf_op | source)
XLA Modules:
  0.0 71.5 jit_solution(16686382607060872528)
XLA Ops:
  0.6 0.8 %copy.8.refs_4_ = f32[4,2]{1,0:T(4,128)S(1)} copy(f32[4,2]{0,1:T(2,128)} %param.9) | data formatting | bytes 64 | tf_op args[4]
  1.4 0.0 copy-start
  1.4 0.9 %copy-done = f32[3,4,16,128]{3,2,1,0:T(8,128)S(1)} copy-done((f32[3,4,16,128]{3,2,1,0:T(8,128)S(1)}, f32[3,4,16,128]{3,2,1,0:T(8,128)}, u32[]{:S(2)}) %copy-start) | copy-done | bytes 98328
  2.3 0.0 copy-start.1
  2.3 0.8 %copy-done.1 = s32[4,16,128]{2,1,0:T(8,128)S(1)} copy-done((s32[4,16,128]{2,1,0:T(8,128)S(1)}, s32[4,16,128]{2,1,0:T(8,128)}, u32[]{:S(2)}) %copy-start.1) | copy-done | bytes 32792
  3.0 0.0 copy-start.2
  3.0 0.8 %copy-done.2 = f32[4,16,128]{2,1,0:T(8,128)S(1)} copy-done((f32[4,16,128]{2,1,0:T(8,128)S(1)}, f32[4,16,128]{2,1,0:T(8,128)}, u32[]{:S(2)}) %copy-start.2) | copy-done | bytes 32792
  3.8 0.0 copy-start.3
  3.8 0.8 %copy-done.3 = s32[4,16,128]{2,1,0:T(8,128)S(1)} copy-done((s32[4,16,128]{2,1,0:T(8,128)S(1)}, s32[4,16,128]{2,1,0:T(8,128)}, u32[]{:S(2)}) %copy-start.3) | copy-done | bytes 32792
  4.6 65.2 %shard_map.76 = (f32[3,4,16,128]{3,2,1,0:T(8,128)S(1)}, f32[3,4,16,128]{3,2,1,0:T(8,128)S(1)}, f32[6]{0:T(128)S(1)}) custom-call(f32[3,4,16,128]{3,2,1,0:T(8,128)S(1)} %copy-done, s32[4,16,128]{2,1,0:T(8,128)S(1)} %copy-done.1, f32[4,16,128]{2,1,0:T(8,128)S(1)} %copy-done.2, s32[4,16,128]{2,1,0:T(8,128)S(1)} %copy-done.3, f32[4,2]{1,0:T(4,128)S(1)} %copy.8.refs_4_), custom_call_target="tpu_custom_call" | custom-call | tf_op jit(solution)/shard_map/pallas_call | solution.py:367
  69.7 0.6 copy.12
  70.4 0.6 copy.13
  71.0 0.5 copy.14
Async XLA Ops:
  1.4 0.9 %copy-start = (f32[3,4,16,128]{3,2,1,0:T(8,128)S(1)}, f32[3,4,16,128]{3,2,1,0:T(8,128)}, u32[]{:S(2)}) copy-start(f32[3,4,16,128]{3,2,1,0:T(8,128)} %refs_0_.1) | copy-start | bytes 294916
  2.3 0.8 %copy-start.1 = (s32[4,16,128]{2,1,0:T(8,128)S(1)}, s32[4,16,128]{2,1,0:T(8,128)}, u32[]{:S(2)}) copy-start(s32[4,16,128]{2,1,0:T(8,128)} %refs_1_.1) | copy-start | bytes 98308
  3.0 0.8 %copy-start.2 = (f32[4,16,128]{2,1,0:T(8,128)S(1)}, f32[4,16,128]{2,1,0:T(8,128)}, u32[]{:S(2)}) copy-start(f32[4,16,128]{2,1,0:T(8,128)} %refs_2_.1) | copy-start | bytes 98308
  3.8 0.8 %copy-start.3 = (s32[4,16,128]{2,1,0:T(8,128)S(1)}, s32[4,16,128]{2,1,0:T(8,128)}, u32[]{:S(2)}) copy-start(s32[4,16,128]{2,1,0:T(8,128)} %refs_3_.1) | copy-start | bytes 98308
where the time goes:
time: 71.9 us; the launch traced here: 71.5 us
  Pallas kernels  65.2 us (91%)
  local copies, waits for them, and re-layouts  5.72 us (8%)
    pallas_call x1, Pallas kernels, shards(): pl.pallas_call(kernel, out_shape=(jax.ShapeDtypeStruct(body_load.shape, j...  65.2 us
    unnamed x12, local copies, waits for them, and re-layouts  5.72 us

commit v1 on v0

v1 whole, which is shorter than its diff:
```python
import functools

import jax
import jax.numpy as jnp
import numpy as np
from jax import lax
from jax.experimental import pallas as pl
from jax.experimental.pallas import tpu as pltpu
from jax.sharding import PartitionSpec as P

ITERS = 6
DEPTHS = (3, 2)
AXES = ("gx", "gy", "gz")
MESH = pl.DeviceIdType.MESH


def corner_offsets(a):
    return (a >> 2 & 1, a >> 1 & 1, a & 1)


def element_tables():
    points = np.array([(1.0 - 3.0 ** (-0.5)) / 2.0, (1.0 + 3.0 ** (-0.5)) / 2.0])
    stiff_lame = np.zeros((24, 24))
    stiff_shear = np.zeros((24, 24))
    for p in points:
        for q in points:
            for r in points:
                position = (p, q, r)
                gradients = np.zeros((8, 3))
                for a in range(8):
                    corner = corner_offsets(a)
                    for d in range(3):
                        factor = 1.0
                        for e in range(3):
                            if e == d:
                                factor = factor * (1.0 if corner[e] else -1.0)
                            else:
                                factor = factor * (position[e] if corner[e] else 1.0 - position[e])
                        gradients[a, d] = factor
                for a in range(8):
                    for c in range(3):
                        for b in range(8):
                            for d in range(3):
                                stiff_lame[3 * a + c, 3 * b + d] += 0.125 * gradients[a, c] * gradients[b, d]
                                stiff_shear[3 * a + c, 3 * b + d] += 0.125 * (
                                    float(c == d) * np.dot(gradients[a], gradients[b])
                                    + gradients[a, d] * gradients[b, c]
                                )
    return (stiff_lame, stiff_shear)


def element_modes(m, L, M):
    x, y, z = m
    M2 = M + M
    L3 = L * (1.0 / 3.0)
    M3 = M * (1.0 / 3.0)
    Q = (L + (M2 + M2)) * (1.0 / 9.0)
    s = L * (x["DSS"] + y["SDS"] + z["SSD"])
    fx, fy, fz = {}, {}, {}
    fx["DSS"] = s + M2 * x["DSS"]
    fy["SDS"] = s + M2 * y["SDS"]
    fz["SSD"] = s + M2 * z["SSD"]
    fy["DSS"] = fx["SDS"] = M * (y["DSS"] + x["SDS"])
    fz["DSS"] = fx["SSD"] = M * (z["DSS"] + x["SSD"])
    fz["SDS"] = fy["SSD"] = M * (z["SDS"] + y["SSD"])
    ax = L3 * (y["DDS"] + z["DSD"])
    ay = L3 * (x["DDS"] + z["SDD"])
    az = L3 * (x["DSD"] + y["SDD"])
    fx["DDS"] = ay + M * x["DDS"]
    fx["DSD"] = az + M * x["DSD"]
    fy["DDS"] = ax + M * y["DDS"]
    fy["SDD"] = az + M * y["SDD"]
    fz["DSD"] = ax + M * z["DSD"]
    fz["SDD"] = ay + M * z["SDD"]
    p = M3 * (y["DSD"] + x["SDD"])
    q = M3 * (x["SDD"] + z["DDS"])
    r = M3 * (y["DSD"] + z["DDS"])
    fx["SDD"] = p + q
    fy["DSD"] = p + r
    fz["DDS"] = q + r
    for f, v in ((fx, x), (fy, y), (fz, z)):
        f["DDD"] = Q * v["DDD"]
    return fx, fy, fz


YZ = ("SS", "SD", "DS", "DD")


def plane_modes(v):
    rows, lanes = v.shape
    nz = pltpu.roll(v, lanes - 1, 1)
    s, d = v + nz, nz - v
    s1, d1 = pltpu.roll(s, rows - 1, 0), pltpu.roll(d, rows - 1, 0)
    return [s + s1, d + d1, s1 - s, d1 - d]


def plane_forces(g):
    B = []
    for zm in (0, 1):
        S, D = g[zm], g[2 + zm]
        B.append((S - D) + pltpu.roll(S + D, 1, 0))
    return (B[0] - B[1]) + pltpu.roll(B[0] + B[1], 1, 1)


def make_kernel(counts, brick, nmat, gl, gm):
    bx, by, bz = brick
    H = max(DEPTHS)
    rounds = len(DEPTHS)
    total = counts[0] * counts[1] * counts[2]
    nfields = [5] + [3] * (rounds - 1)
    YW = by + 8
    ZW = 2 * bz
    slots = min(counts[0], 3)
    xdirs = (0, 1) if counts[0] == 2 else (0, 1, -1)
    dirs = [(dx, dy, dz) for dx in xdirs for dy in (-1, 0, 1) for dz in (-1, 0, 1)][0:]
    dirs = [k for k in dirs if k != (0, 0, 0)]
    dirs.sort(key=lambda k: -sum(abs(a) for a in k))
    ytiles = [-(-n * d // 8) * 8 for n, d in zip(nfields, DEPTHS)]
    group = [max(1, bz // (2 * d * n)) for n, d in zip(nfields, DEPTHS)]
    ztiles = [-(-bx // g) for g in group]

    def kernel(*refs):
        body, mask_in, gap_in, mat_in, lame, u_out, w_out, gap_out = refs[:8]
        Rs, YSs, YBs, ZBs = (refs[8 + i * rounds : 8 + (i + 1) * rounds] for i in range(4))
        (U, W, N, B, LOW, LL, MM, GA, GT, GR, mask, gap, mat, send, recv, gsend, grecv, isem) = refs[8 + 4 * rounds :]
        me = [lax.axis_index(a) for a in AXES]
        around = [[lax.rem(me[i] + k, counts[i]) for k in range(counts[i])] for i in range(3)]

        def peer(offset):
            return tuple(around[i][offset[i] % counts[i]] for i in range(3))

        def everyone(act):
            if total <= 64:
                for j in range(1, total):
                    a, b = j // (counts[1] * counts[2]), (j // counts[2]) % counts[1]
                    act(j - 1, peer((a, b, j % counts[2])))
            else:

                @pl.loop(1, total)
                def _(j):
                    step = (j // (counts[1] * counts[2]), (j // counts[2]) % counts[1], j % counts[2])
                    act(j - 1, tuple(lax.rem(me[i] + step[i], counts[i]) for i in range(3)))

        barrier = pltpu.get_barrier_semaphore()
        loads = [
            pltpu.make_async_copy(body, Rs[0].at[pl.ds(0, 3), pl.ds(0, bx)], isem.at[0]),
            pltpu.make_async_copy(mask_in, mask, isem.at[1]),
            pltpu.make_async_copy(gap_in, gap, isem.at[2]),
            pltpu.make_async_copy(mat_in, mat, isem.at[3]),
        ]
        for load in loads:
            load.start()
        everyone(lambda j, who: pl.semaphore_signal(barrier, inc=1, device_id=who, device_id_type=MESH))

        lane = lax.broadcasted_iota(jnp.int32, (by, bz), 1)
        lane8 = lax.broadcasted_iota(jnp.int32, (YW, bz), 1)

        def fill(r):
            d, n = DEPTHS[r], nfields[r]
            for tile in range(ztiles[r]):
                packed = None
                for x in range(tile * group[r], min(bx, (tile + 1) * group[r])):
                    for f in range(n):
                        v = Rs[r][f, x]
                        YSs[r][0, x, f * d : f * d + d, :] = v[by - d :]
                        YSs[r][1, x, f * d : f * d + d, :] = v[:d]
                        at = 2 * d * ((x - tile * group[r]) * n + f)
                        shifted = pltpu.roll(v, (at + d) % bz, 1)
                        packed = shifted if packed is None else jnp.where(lane >= at, shifted, packed)
                ZBs[r][0, 0, tile, 8 : 8 + by, :] = packed

        def copies(r):
            for k, (dx, dy, dz) in enumerate(dirs):
                slot = 0 if dx == 0 else (1 if dx < 0 or counts[0] == 2 else 2)
                planes = pl.ds(slot * bx, bx)
                if dz != 0:
                    sy = pl.ds(by, 8) if dy > 0 else pl.ds(8, 8 if dy else by)
                    ty = pl.ds(0, 8) if dy > 0 else (pl.ds(8 + by, 8) if dy else pl.ds(8, by))
                    src = ZBs[r].at[0, 0, :, sy, :]
                    dst = ZBs[r].at[1 if dz > 0 else 2, slot, :, ty, :]
                elif dy != 0:
                    side = 0 if dy > 0 else 1
                    src, dst = YSs[r].at[side], YBs[r].at[side, planes]
                else:
                    src, dst = Rs[r].at[:, pl.ds(0, bx)], Rs[r].at[:, planes]
                yield pltpu.make_async_remote_copy(
                    src_ref=src,
                    dst_ref=dst,
                    send_sem=send.at[r, k],
                    recv_sem=recv.at[r, k],
                    device_id=peer((dx, dy, dz)),
                    device_id_type=MESH,
                )

        def unpack(r, targets):
            d, n = DEPTHS[r], nfields[r]
            for x in range(H - d, H + bx + d):
                at = (x - H) % (slots * bx)
                slot, p = at // bx, at % bx
                tile = p // group[r]
                rows = pl.ds(4, YW)
                both = jnp.where(
                    lane8 % (2 * d) < d, ZBs[r][1, slot, tile, rows, :], ZBs[r][2, slot, tile, rows, :]
                )
                for f, put in enumerate(targets):
                    o = put(x)
                    if r == 0 or slot != 0:
                        o[4 : 4 + by, :bz] = Rs[r][f, at]
                    o[4 - d : 4, :bz] = YBs[r][0, at, f * d : f * d + d, :]
                    o[4 + by : 4 + by + d, :bz] = YBs[r][1, at, f * d : f * d + d, :]
                    shift = 2 * d * ((p - tile * group[r]) * n + f) + d
                    o[:, bz:] = pltpu.roll(both, (bz - shift) % bz, 1)

        top = None
        for m in range(nmat):
            row = lame[0, m] * gl + lame[1, m] * gm
            top = row if top is None else jnp.maximum(top, row)
        tau = 1.5 / jnp.full((YW, ZW), 1.0 + 8.0 * top, jnp.float32)

        for load in loads:
            load.wait()
        for x in range(bx):
            Rs[0][3, x] = jnp.where(mask[x] > 0, -gap[x], -jnp.inf)
            Rs[0][4, x] = mat[x].astype(jnp.float32)
        fill(0)
        GT[...] = jnp.zeros_like(GT)
        pl.semaphore_wait(barrier, total - 1)

        def settle(x, u, w, low):
            worst = None
            for c in range(3):
                v = u[c] + w[c]
                z = jnp.maximum(v, low) if c == 2 else v
                wc = v - z
                res = u[c] - z
                W[c, x], N[c, x] = wc, res + wc
                a = jnp.abs(res[:, :bz])
                worst = a if worst is None else jnp.maximum(worst, a)
            inside = jnp.logical_and(x >= H, x < H + bx)
            GA[...] = jnp.maximum(GA[...], jnp.where(inside, worst, 0.0))

        def record(t):
            GT[t : t + 1, :] = jnp.max(GA[4 : 4 + by, :], axis=0, keepdims=True)
            GA[...] = jnp.zeros_like(GA)

        GA[...] = jnp.zeros_like(GA)
        t = 0
        for r, d in enumerate(DEPTHS):
            if r > 0:
                for c in range(3):
                    for x in range(bx):
                        Rs[r][c, x] = U[c, H + x, 4 : 4 + by, :bz]
                fill(r)
            for copy in copies(r):
                copy.start()
            for copy in copies(r):
                copy.wait_recv()
            if r == 0:
                unpack(0, [lambda x, c=c: B.at[c, x] for c in range(3)] + [lambda x: LOW.at[x], lambda x: LL.at[x]])

                @pl.loop(0, bx + 2 * H)
                def _(x):
                    u = []
                    for c in range(3):
                        b = tau * B[c, x]
                        B[c, x] = b
                        U[c, x] = b
                        u.append(b)
                    kind = LL[x]
                    first = jnp.zeros_like(kind)
                    shear = jnp.zeros_like(kind)
                    for m in range(nmat):
                        hit = kind == float(m)
                        first = jnp.where(hit, lame[0, m], first)
                        shear = jnp.where(hit, lame[1, m], shear)
                    LL[x] = first * (tau * 0.0625)
                    MM[x] = shear * (tau * 0.0625)
                    zero = jnp.zeros_like(kind)
                    settle(x, u, [zero, zero, zero], LOW[x])

            else:
                unpack(r, [lambda x, c=c: U.at[c, x] for c in range(3)])

                @pl.loop(H - d + 1, H + bx + d - 1)
                def _(x):
                    settle(x, [U[c, x] for c in range(3)], [W[c, x] for c in range(3)], LOW[x])

            record(t)
            t += 1
            for left in range(d, 0, -1):
                start = H - left
                final = left > 1 or r == rounds - 1

                def step(e, carry):
                    prev, hi = carry
                    cur = [plane_modes(U[c, e + 1]) for c in range(3)]
                    modes = []
                    for c in range(3):
                        m = {}
                        for i, yz in enumerate(YZ):
                            a, b = prev[4 * c + i], cur[c][i]
                            m["D" + yz] = b - a
                            if yz != "SS":
                                m["S" + yz] = a + b
                        modes.append(m)
                    forces = element_modes(modes, LL[e], MM[e])
                    new_hi, u = [], []
                    for c in range(3):
                        g = []
                        for i, yz in enumerate(YZ):
                            D = forces[c]["D" + yz]
                            h = hi[4 * c + i]
                            if yz == "SS":
                                g.append(h - D)
                                new_hi.append(D)
                            else:
                                S = forces[c]["S" + yz]
                                g.append(h + (S - D))
                                new_hi.append(S + D)
                        F = plane_forces(g)
                        u.append(U[c, e] - ((F - B[c, e]) + tau * N[c, e]))
                        U[c, e] = u[c]
                    if final:
                        settle(e, u, [W[c, e] for c in range(3)], LOW[e])
                    return [v for c in cur for v in c], new_hi

                zero = jnp.zeros((YW, ZW), jnp.float32)
                carry = ([v for c in range(3) for v in plane_modes(U[c, start])], [zero] * 12)
                lax.fori_loop(start, H + bx - 1 + left, step, carry, unroll=True)
                if final:
                    record(t)
                    t += 1

        def spread(j, who):
            return pltpu.make_async_remote_copy(
                src_ref=GT,
                dst_ref=GR.at[j],
                send_sem=gsend,
                recv_sem=grecv,
                device_id=who,
                device_id_type=MESH,
            )

        everyone(lambda j, who: spread(j, who).start())
        for c in range(3):
            for x in range(bx):
                u_out[c, x] = U[c, H + x, 4 : 4 + by, :bz]
                w_out[c, x] = W[c, H + x, 4 : 4 + by, :bz]
        for r in range(rounds):
            for copy in copies(r):
                copy.wait_send()
        whole = pltpu.make_async_remote_copy(
            src_ref=GR,
            dst_ref=GR,
            send_sem=gsend,
            recv_sem=grecv,
            device_id=peer((0, 0, 1)),
            device_id_type=MESH,
        )
        whole.wait_recv()
        worst = jnp.maximum(GT[...], jnp.max(GR[...], axis=0))
        for i in range(ITERS):
            gap_out[i] = jnp.max(worst[i : i + 1, :])
        whole.wait_send()

    X = bx + 2 * H
    buffer = lambda *dims: pltpu.VMEM(dims, jnp.float32)
    scratch = [buffer(n, slots * bx, by, bz) for n in nfields]
    scratch += [buffer(2, bx, rows, bz) for rows in ytiles]
    scratch += [buffer(2, slots * bx, rows, bz) for rows in ytiles]
    scratch += [buffer(3, slots, tiles, by + 16, bz) for tiles in ztiles]
    scratch += [buffer(3, X, YW, ZW)] * 4 + [buffer(X, YW, ZW)] * 3
    scratch += [
        buffer(YW, bz),
        buffer(8, bz),
        buffer(total - 1, 8, bz),
        pltpu.VMEM((bx, by, bz), jnp.int32),
        buffer(bx, by, bz),
        pltpu.VMEM((bx, by, bz), jnp.int32),
        pltpu.SemaphoreType.DMA((rounds, len(dirs))),
        pltpu.SemaphoreType.DMA((rounds, len(dirs))),
        pltpu.SemaphoreType.DMA,
        pltpu.SemaphoreType.DMA,
        pltpu.SemaphoreType.DMA((4,)),
    ]
    return kernel, scratch


def shards(counts, body_load, contact_mask, contact_gap, material_ids, lame_table):
    stiff_lame, stiff_shear = element_tables()
    gl = float(np.max(np.sum(np.abs(stiff_lame), 1)))
    gm = float(np.max(np.sum(np.abs(stiff_shear), 1)))
    kernel, scratch = make_kernel(counts, material_ids.shape, lame_table.shape[0], gl, gm)
    vmem = pl.BlockSpec(memory_space=pltpu.VMEM)
    anywhere = pl.BlockSpec(memory_space=pltpu.HBM)
    smem = pl.BlockSpec(memory_space=pltpu.SMEM)
    return pl.pallas_call(
        kernel,
        out_shape=(
            jax.ShapeDtypeStruct(body_load.shape, jnp.float32),
            jax.ShapeDtypeStruct(body_load.shape, jnp.float32),
            jax.ShapeDtypeStruct((ITERS,), jnp.float32),
        ),
        in_specs=[anywhere] * 4 + [smem],
        out_specs=(vmem, vmem, smem),
        scratch_shapes=scratch,
        compiler_params=pltpu.CompilerParams(
            collective_id=0, has_side_effects=True, vmem_limit_bytes=62 * 1024 * 1024
        ),
    )(body_load, contact_mask, contact_gap, material_ids, lame_table.T)


def solution(mesh):
    counts = tuple(mesh.shape[a] for a in AXES)
    in_specs = (
        P(None, "gx", "gy", "gz"),
        P("gx", "gy", "gz"),
        P("gx", "gy", "gz"),
        P("gx", "gy", "gz"),
        P(),
    )
    out_specs = (P(None, "gx", "gy", "gz"), P(None, "gx", "gy", "gz"), P())
    return jax.shard_map(
        functools.partial(shards, counts), mesh=mesh, in_specs=in_specs, out_specs=out_specs, check_vma=False
    )
```

time: 71.9 us -> 38 us (0.53)
  Pallas kernels: 65.2 us -> 34.4 us
  local copies, waits for them, and re-layouts: 5.72 us -> 2.73 us
    pallas_call x1, Pallas kernels: 65.2 us -> 34.4 us  [shards(): pl.pallas_call(kernel, out_shape=(jax.ShapeDtypeStruct(body_load.shape, j...]
    unnamed x12 -> x7, local copies, waits for them, and re-layouts: 5.72 us -> 2.73 us
where the time goes in v1:
time: 38 us; the launch traced here: 37.8 us
  Pallas kernels  34.4 us (91%)
  local copies, waits for them, and re-layouts  2.73 us (7%)
  between operations  0.65 us (2%)
    pallas_call x1, Pallas kernels, shards(): pl.pallas_call(kernel, out_shape=(jax.ShapeDtypeStruct(body_load.shape, j...  34.4 us
    unnamed x7, local copies, waits for them, and re-layouts  2.73 us

profile of v1, /device:TPU:0, one launch (start us, length us, event | category | flops | bytes accessed | tf_op | source)
XLA Modules:
  0.0 37.8 jit_solution(3905515790183106941)
XLA Ops:
  0.6 34.4 %shard_map.76 = (f32[3,4,16,128]{3,2,1,0:T(8,128)}, f32[3,4,16,128]{3,2,1,0:T(8,128)}, f32[6]{0:T(128)}) custom-call(f32[3,4,16,128]{3,2,1,0:T(8,128)} %refs_0_.1, s32[4,16,128]{2,1,0:T(8,128)} %refs_1_.1, f32[4,16,128]{2,1,0:T(8,128)} %refs_2_.1, s32[4,16,128]{2,1,0:T(8,128)} %refs_3_.1, f32[2,4]{1,0:T(2,128)} %bitcast.1), custom_call_target="tpu_custom_call" | custom-call | tf_op jit(solution)/shard_map/pallas_call | solution.py:397
  35.1 0.0 copy-start
  35.1 1.6 %copy.11 = f32[3,4,16,128]{3,2,1,0:T(8,128)} copy(f32[3,4,16,128]{3,2,1,0:T(8,128)} %get-tuple-element.6) | data formatting | bytes 196608
  36.6 0.0 copy-done
  36.6 0.0 copy-start.1
  36.6 0.6 %copy.12 = f32[3,4,16,128]{3,2,1,0:T(8,128)} copy(f32[3,4,16,128]{3,2,1,0:T(8,128)S(1)} %copy-done) | data formatting | bytes 196608
  37.3 0.0 copy-done.1
  37.3 0.5 %copy.13 = f32[6]{0:T(128)} copy(f32[6]{0:T(128)S(1)} %copy-done.1) | data formatting | bytes 48
Async XLA Ops:
  35.1 1.6 %copy-start = (f32[3,4,16,128]{3,2,1,0:T(8,128)S(1)}, f32[3,4,16,128]{3,2,1,0:T(8,128)}, u32[]{:S(2)}) copy-start(f32[3,4,16,128]{3,2,1,0:T(8,128)} %get-tuple-element.7) | copy-start | bytes 294916
  36.6 0.6 %copy-start.1 = (f32[6]{0:T(128)S(1)}, f32[6]{0:T(128)}, u32[]{:S(2)}) copy-start(f32[6]{0:T(128)} %get-tuple-element.8) | copy-start | bytes 76

commit v2 on v1

--- a/solution.py
+++ b/solution.py
@@ -120,9 +120,9 @@
     ztiles = [-(-bx // g) for g in group]
 
     def kernel(*refs):
-        body, mask_in, gap_in, mat_in, lame, u_out, w_out, gap_out = refs[:8]
+        body, mask_in, gap_in, mat_in, lame_in, u_out, w_out, gap_out = refs[:8]
         Rs, YSs, YBs, ZBs = (refs[8 + i * rounds : 8 + (i + 1) * rounds] for i in range(4))
-        (U, W, N, B, LOW, LL, MM, GA, GT, GR, mask, gap, mat, send, recv, gsend, grecv, isem) = refs[8 + 4 * rounds :]
+        (U, W, N, B, LOW, LL, MM, GA, GT, GR, mask, gap, mat, lame, send, recv, gsend, grecv, isem) = refs[8 + 4 * rounds :]
         me = [lax.axis_index(a) for a in AXES]
         around = [[lax.rem(me[i] + k, counts[i]) for k in range(counts[i])] for i in range(3)]
 
@@ -131,7 +131,7 @@
 
         def everyone(act):
             if total <= 64:
-                for j in range(1, total):
+                for j in range(total - 1, 0, -1):
                     a, b = j // (counts[1] * counts[2]), (j // counts[2]) % counts[1]
                     act(j - 1, peer((a, b, j % counts[2])))
             else:
@@ -147,6 +147,7 @@
             pltpu.make_async_copy(mask_in, mask, isem.at[1]),
             pltpu.make_async_copy(gap_in, gap, isem.at[2]),
             pltpu.make_async_copy(mat_in, mat, isem.at[3]),
+            pltpu.make_async_copy(lame_in, lame, isem.at[4]),
         ]
         for load in loads:
             load.start()
@@ -211,14 +212,14 @@
                     shift = 2 * d * ((p - tile * group[r]) * n + f) + d
                     o[:, bz:] = pltpu.roll(both, (bz - shift) % bz, 1)
 
+        for load in loads:
+            load.wait()
         top = None
         for m in range(nmat):
             row = lame[0, m] * gl + lame[1, m] * gm
             top = row if top is None else jnp.maximum(top, row)
         tau = 1.5 / jnp.full((YW, ZW), 1.0 + 8.0 * top, jnp.float32)
 
-        for load in loads:
-            load.wait()
         for x in range(bx):
             Rs[0][3, x] = jnp.where(mask[x] > 0, -gap[x], -jnp.inf)
             Rs[0][4, x] = mat[x].astype(jnp.float32)
@@ -377,11 +378,12 @@
         pltpu.VMEM((bx, by, bz), jnp.int32),
         buffer(bx, by, bz),
         pltpu.VMEM((bx, by, bz), jnp.int32),
+        pltpu.SMEM((2, nmat), jnp.float32),
         pltpu.SemaphoreType.DMA((rounds, len(dirs))),
         pltpu.SemaphoreType.DMA((rounds, len(dirs))),
         pltpu.SemaphoreType.DMA,
         pltpu.SemaphoreType.DMA,
-        pltpu.SemaphoreType.DMA((4,)),
+        pltpu.SemaphoreType.DMA((5,)),
     ]
     return kernel, scratch
 
@@ -401,7 +403,7 @@
             jax.ShapeDtypeStruct(body_load.shape, jnp.float32),
             jax.ShapeDtypeStruct((ITERS,), jnp.float32),
         ),
-        in_specs=[anywhere] * 4 + [smem],
+        in_specs=[anywhere] * 5,
         out_specs=(vmem, vmem, smem),
         scratch_shapes=scratch,
         compiler_params=pltpu.CompilerParams(

time: 38 us -> 37.1 us (0.976)
  Pallas kernels: 34.4 us -> 33.5 us
    pallas_call x1, Pallas kernels: 34.4 us -> 33.5 us  [shards(): pl.pallas_call(kernel, out_shape=(jax.ShapeDtypeStruct(body_load.shape, j...]
where the time goes in v2:
time: 37.1 us; the launch traced here: 36.9 us
  Pallas kernels  33.5 us (90%)
  local copies, waits for them, and re-layouts  2.73 us (7%)
  between operations  0.65 us (2%)
    pallas_call x1, Pallas kernels, shards(): pl.pallas_call(kernel, out_shape=(jax.ShapeDtypeStruct(body_load.shape, j...  33.5 us
    unnamed x7, local copies, waits for them, and re-layouts  2.73 us

profile of v2, /device:TPU:0, one launch (start us, length us, event | category | flops | bytes accessed | tf_op | source)
XLA Modules:
  0.0 36.9 jit_solution(13083108630592984236)
XLA Ops:
  0.6 33.5 %shard_map.76 = (f32[3,4,16,128]{3,2,1,0:T(8,128)}, f32[3,4,16,128]{3,2,1,0:T(8,128)}, f32[6]{0:T(128)}) custom-call(f32[3,4,16,128]{3,2,1,0:T(8,128)} %refs_0_.1, s32[4,16,128]{2,1,0:T(8,128)} %refs_1_.1, f32[4,16,128]{2,1,0:T(8,128)} %refs_2_.1, s32[4,16,128]{2,1,0:T(8,128)} %refs_3_.1, f32[2,4]{1,0:T(2,128)} %bitcast.1), custom_call_target="tpu_custom_call" | custom-call | tf_op jit(solution)/shard_map/pallas_call | solution.py:399
  34.2 0.0 copy-start
  34.2 1.6 %copy.11 = f32[3,4,16,128]{3,2,1,0:T(8,128)} copy(f32[3,4,16,128]{3,2,1,0:T(8,128)} %get-tuple-element.6) | data formatting | bytes 196608
  35.8 0.0 copy-done
  35.8 0.0 copy-start.1
  35.8 0.6 %copy.12 = f32[3,4,16,128]{3,2,1,0:T(8,128)} copy(f32[3,4,16,128]{3,2,1,0:T(8,128)S(1)} %copy-done) | data formatting | bytes 196608
  36.4 0.0 copy-done.1
  36.4 0.5 %copy.13 = f32[6]{0:T(128)} copy(f32[6]{0:T(128)S(1)} %copy-done.1) | data formatting | bytes 48
Async XLA Ops:
  34.2 1.6 %copy-start = (f32[3,4,16,128]{3,2,1,0:T(8,128)S(1)}, f32[3,4,16,128]{3,2,1,0:T(8,128)}, u32[]{:S(2)}) copy-start(f32[3,4,16,128]{3,2,1,0:T(8,128)} %get-tuple-element.7) | copy-start | bytes 294916
  35.8 0.6 %copy-start.1 = (f32[6]{0:T(128)S(1)}, f32[6]{0:T(128)}, u32[]{:S(2)}) copy-start(f32[6]{0:T(128)} %get-tuple-element.8) | copy-start | bytes 76
